TPU v7x, 256 devices: a whole 4x4x8 slice. The times are simulated.
256 devices in a mesh: segment: 16 (over z, x_lo), dp: 16 (over y, x_hi, core).
Axes of the slice: x: 4 (x_hi: 2, x_lo: 2; x = x_hi * 2 + x_lo), y: 4, z: 8, core: 2. Of those that a mesh axis runs over, the one named last changes fastest.
Arguments:
- src_embed: bfloat16 [64, 128, 2048], P('dp', None, 'segment'), parts along dimension 0, may hold values from -6 to 6
- tgt_embed: bfloat16 [64, 128, 2048], P('dp', None, 'segment'), parts along dimension 0, may hold values from -6 to 6
- src_lengths: int32 [64], P('dp'), parts along dimension 0, may hold values from 32 to 128
- tgt_lengths: int32 [64], P('dp'), parts along dimension 0, may hold values from 32 to 128
- attn_in: bfloat16 [16, 2048, 1536], P('segment'), may hold values from -0.125 to 0.125
- attn_out: bfloat16 [16, 512, 2048], P('segment'), may hold values from -0.375 to 0.375
- norm_gain: float32 [4, 2048], replicated, may hold values from 0.25 to 1.75
- final_gain: float32 [2048], replicated, may hold values from 0.25 to 1.75
Outputs:
- decoded: bfloat16 [64, 128, 2048], P('dp', None, 'segment'), parts along dimension 0
There are 16 independent parts, one for each index of `dp`. A program takes and returns all parts, laid end to end along the dimension named above; an argument that names none is the same for every part. Nothing has to cross between parts.
Inputs may be any that keep to these rules, and one draw needn't show every extreme that they name: `src_lengths`: keys at positions below a sequence's length are its real tokens. `tgt_lengths`: keys at positions below a sequence's length are its real tokens.
All inputs are finite; a program needn't handle non-finite values.
Results may differ from a plain program's by a relative error of at most 0.015.
Values may be sent and summed in bfloat16 or wider, within the bound.
A program may use at most 64 MiB of HBM per device.

v0:
```python
import functools

import jax
import jax.numpy as jnp
from jax import lax
from jax.experimental import pallas as pl
from jax.experimental.pallas import tpu as pltpu
from jax.sharding import PartitionSpec as P

HEAD = 64
GROUP = 4
CHUNKS = 4
AHEAD = 1
EARLY = 0
EPS = 1e-06
SCALE = 0.125
MASKED = -1000000000.0
MESH = pl.DeviceIdType.MESH
F32 = jnp.float32
BF16 = jnp.bfloat16


def rms(values, gain):
    return values * lax.rsqrt(jnp.mean(values * values, axis=-1, keepdims=True) + EPS) * gain


def kernel(
    n_seg, n_dp, src, tgt, slen, tlen, win, wout, gain, fgain, out,
    w_in, w_out, w_far, lens_own, lens_far, lens, arr, tg, nb, qs, qkv, mix, mix_far, pf, part, rx, rz, zs, yb,
    wsem, lens_s, lens_r, far_s, far_r, mix_s, mix_r, src_s, tgt_s, src_r, tgt_r, tz_s, tz_r, tx_s, tx_r,
    relay_s, relay_r, agz_s, agz_r, agx_s, agx_r, rsx_s, rsx_r, rsz_s, rsz_r, out_s, out_r,
):
    batches, seq, cols = src.shape
    rows = seq // GROUP
    half = seq // 2
    block = cols * n_seg // CHUNKS
    heads = w_out.shape[0]
    s = lax.axis_index("segment")
    sect = s // GROUP
    m = s % GROUP
    zl = m // 2
    xl = m % 2
    x_near = s + 1 - 2 * xl
    d = lax.axis_index("dp")
    flipped = d + 2 - 4 * ((d // 2) % 2)
    alt = d % 2 == 1
    swap = alt & (xl == 0)
    x_dp = jnp.where(alt, flipped, d)
    work_dp = jnp.where(swap, flipped, d)
    core = d % 2
    twin = d + 1 - 2 * core
    own_q = xl * 2 + zl
    z_q = xl * 2 + 1 - zl
    lower = (sect > 0) & (zl == 0)
    upper = (sect > 0) & (zl == 1)
    z_near = s + 2 - 4 * zl
    last = n_seg // GROUP - 1

    load_in = pltpu.make_async_copy(win.at[0], w_in, wsem.at[0])
    load_out = pltpu.make_async_copy(wout.at[0], w_out, wsem.at[1])
    load_in.start()
    load_out.start()

    barrier = pltpu.get_barrier_semaphore()
    for k in range(1, n_seg):
        pl.semaphore_signal(
            barrier, inc=1, device_id={"segment": (s + k) % n_seg}, device_id_type=MESH
        )

    pl.semaphore_signal(
        barrier, inc=1, device_id={"segment": s, "dp": twin}, device_id_type=MESH
    )

    for k in range(1, n_dp // 4):
        pl.semaphore_signal(
            barrier, inc=1, device_id={"segment": s, "dp": (d + 4 * k) % n_dp}, device_id_type=MESH
        )

    @pl.when(alt)
    def _():
        for k in range(n_seg):
            pl.semaphore_signal(
                barrier, inc=1, device_id={"segment": k, "dp": flipped}, device_id_type=MESH
            )

    row = lax.broadcasted_iota(jnp.int32, lens_own.shape, 0)
    table = jnp.zeros(lens_own.shape, F32)
    for k in range(batches):
        table = jnp.where(row == k, slen[k].astype(F32), table)
        table = jnp.where(row == batches + k, tlen[k].astype(F32), table)
    lens_own[...] = table
    with jax.named_scope("barrier"):
        pl.semaphore_wait(barrier, n_seg + n_dp // 4 - 1 + jnp.where(alt, n_seg, 0))

    def remote(src_ref, dst_ref, send, recv, target, target_dp=None):
        return pltpu.make_async_remote_copy(
            src_ref=src_ref, dst_ref=dst_ref, send_sem=send, recv_sem=recv,
            device_id={"segment": target, "dp": d if target_dp is None else target_dp},
            device_id_type=MESH,
        )

    def lens_copy():
        return remote(lens_own, lens_far, lens_s, lens_r, s, flipped)

    @pl.when(swap)
    def _():
        lens_copy().start()

    def wait_for(ref, sem):
        pltpu.make_async_copy(ref, ref, sem).wait()

    def quarter(q):
        return pl.ds(pl.multiple_of(q * rows, rows), rows)

    def strip(c):
        return slice(c * block, (c + 1) * block)

    tall = n_dp // 4
    share = heads // (2 * tall)
    y = d // 4

    def far_rows(level):
        return pl.ds(pl.multiple_of((core * tall + level) * share, share), share)

    def far_copy():
        return remote(wout.at[0, far_rows(y)], w_far.at[far_rows(y)], far_s.at[0], far_r.at[0], z_near)

    def far_side(k):
        ref = w_far.at[far_rows(y)]
        return remote(ref, ref, far_s.at[k], far_r.at[k], s, (d + 4 * k) % n_dp)

    def far_swap():
        ref = w_far.at[pl.ds(pl.multiple_of(core * (heads // 2), heads // 2), heads // 2)]
        return remote(ref, ref, far_s.at[tall], far_r.at[tall], s, twin)

    own_cols = pl.ds(pl.multiple_of(s * cols, cols), cols)

    def part_of(t):
        return slice((t % 2 * 2 + t // 2) * rows, (t % 2 * 2 + t // 2 + 1) * rows)

    def spread(given, held, send, recv, first, b, t):
        return remote(
            given.at[b, part_of(t)], held.at[b, part_of(t), own_cols],
            send.at[b, t], recv.at[b], first + t,
            jnp.where(alt, flipped, d) if t % 2 == 0 else d,
        )

    def stays(first, t):
        same = s == first + t
        return same & jnp.logical_not(alt) if t % 2 == 0 else same

    def scatter(given, held, send, recv, first, b):
        for t in range(GROUP):
            @pl.when(jnp.logical_not(stays(first, t)))
            def _():
                spread(given, held, send, recv, first, b, t).start()

            @pl.when(stays(first, t))
            def _():
                pltpu.make_async_copy(
                    given.at[b, part_of(t)], held.at[b, part_of(t), own_cols], recv.at[b]
                ).start()

    def scattered(given, held, send, recv, first, b):
        for t in range(GROUP):
            @pl.when(jnp.logical_not(stays(first, t)))
            def _():
                spread(given, held, send, recv, first, b, t).wait_send()

    def give_source(b, carry):
        scatter(src, arr, src_s, src_r, 0, b)
        return carry

    @pl.when(lower & (sect == 1))
    def _():
        far_copy().start()

    give_source(0, 0)

    @pl.when(sect > 0)
    def _():
        scattered(src, arr, src_s, src_r, 0, 0)

    lax.fori_loop(1, batches, give_source, 0)

    @pl.when(lower & (sect > 1))
    def _():
        far_copy().start()

    def give_target(b, carry):
        scatter(tgt, tg, tgt_s, tgt_r, 2 * GROUP, b)
        return carry

    lax.fori_loop(0, batches, give_target, 0)

    def side_rows(side):
        return pl.ds(pl.multiple_of(side * half, half), half)

    def relay_first(b, c):
        return remote(
            yb.at[b, :rows, strip(c)], arr.at[b, quarter(own_q), strip(c)], relay_s.at[b, c],
            relay_r.at[b, c], GROUP + xl,
        )

    def relay(b, c):
        return remote(
            yb.at[b, :, strip(c)], arr.at[b, side_rows(xl), strip(c)],
            relay_s.at[b, c], relay_r.at[b, c], (s + 2) % n_seg,
        )

    def gather_z(b, c):
        ref = arr.at[b, quarter(own_q), strip(c)]
        return remote(ref, ref, agz_s.at[b, c], agz_r.at[b, c], z_near)

    def gather_x(b, which, c):
        ref = arr.at[b, quarter(own_q if which == 0 else z_q), strip(c)]
        return remote(ref, ref, agx_s.at[b, which, c], agx_r.at[b, which, c], x_near, x_dp)

    def lift_z(b, c):
        ref = arr.at[b, side_rows(xl), strip(c)]
        return remote(ref, ref, agz_s.at[b, c], agz_r.at[b, c], z_near)

    def half_x(b, c):
        ref = arr.at[b, side_rows(xl), strip(c)]
        return remote(ref, ref, agx_s.at[b, 0, c], agx_r.at[b, 0, c], x_near, x_dp)

    def mix_z(b):
        return remote(mix.at[b], mix_far.at[b], mix_s.at[b], mix_r.at[b], z_near)

    def target_z(b):
        ref = tg.at[b, quarter(own_q)]
        return remote(ref, ref, tz_s.at[b], tz_r.at[b], z_near)

    def target_x(b, which):
        ref = tg.at[b, quarter(own_q if which == 0 else z_q)]
        return remote(ref, ref, tx_s.at[b, which], tx_r.at[b, which], x_near, x_dp)

    def sum_x(b, which, c):
        wanted = (1 - xl) * 2 + (1 - zl if which == 0 else zl)
        return remote(
            part.at[b, quarter(wanted), strip(c)], rx.at[b, which * rows:(which + 1) * rows, strip(c)],
            rsx_s.at[b, which, c], rsx_r.at[b, which, c], x_near, x_dp,
        )

    def sum_half(b, c):
        return remote(
            part.at[b, side_rows(1 - xl), strip(c)], rx.at[b, :, strip(c)],
            rsx_s.at[b, 0, c], rsx_r.at[b, 0, c], x_near, x_dp,
        )

    def sum_z(b, c):
        return remote(zs.at[b, :, strip(c)], rz.at[b, :, strip(c)], rsz_s.at[b, c], rsz_r.at[b, c], z_near)

    def out_copy(b, t):
        return remote(
            yb.at[b, :, pl.ds(pl.multiple_of(t * cols, cols), cols)],
            out.at[b, pl.ds(pl.multiple_of(xl * half, half), half)], out_s.at[b, t], out_r.at[b], t, work_dp,
        )

    def step_r(b):
        with jax.named_scope("r_wait"):
            wait_for(arr.at[b, quarter(own_q)], src_r.at[b])
        for c in range(CHUNKS):
            gather_z(b, c).start()
            gather_x(b, 0, c).start()

    def step_f(b, c):
        with jax.named_scope("f_wait"):
            gather_z(b, c).wait_recv()
        gather_x(b, 1, c).start()

    def step_r2(b, c):
        with jax.named_scope("r_wait"):
            wait_for(arr.at[b, side_rows(xl), strip(c)], relay_r.at[b, c])
        lift_z(b, c).start()
        half_x(b, c).start()

    def step_f2(b, c):
        with jax.named_scope("f_wait"):
            lift_z(b, c).wait_recv()
        half_x(b, c).start()

    own_gain = gain[pl.ds(sect, 1), :]

    def attend(b):
        @pl.when(sect == 2)
        def _():
            qkv[:, :heads] = qs[b]
            nb[...] = rms(arr[b].astype(F32), fgain[...]).astype(BF16)

        @pl.when(sect != 2)
        def _():
            nb[...] = rms(arr[b].astype(F32), own_gain).astype(BF16)
            qkv[:, :heads] = jnp.dot(
                nb[...], w_in[:, :heads], preferred_element_type=F32
            ).astype(BF16)

        with jax.named_scope("kv_dot"):
            qkv[:, heads:] = jnp.dot(
                nb[...], w_in[:, heads:], preferred_element_type=F32
            ).astype(BF16)

        length = lens[pl.ds(jnp.where(sect == last, batches, 0) + b, 1), :seq]
        query_pos = lax.broadcasted_iota(jnp.int32, (seq, seq), 0)
        key_pos = lax.broadcasted_iota(jnp.int32, (seq, seq), 1)
        limit = jnp.where(sect == last, query_pos, seq)
        allowed = (key_pos.astype(F32) < length) & (key_pos <= limit)
        allowed = jnp.concatenate([allowed, allowed], axis=0)
        pair = 2 * HEAD
        low = lax.broadcasted_iota(jnp.int32, (seq, pair), 1) < HEAD
        for j in range(heads // pair):
            q2 = qkv[:, j * pair:(j + 1) * pair]
            k2 = qkv[:, heads + j * pair:heads + (j + 1) * pair]
            v2 = qkv[:, 2 * heads + j * pair:2 * heads + (j + 1) * pair]
            zero = jnp.zeros_like(q2)
            stacked = jnp.concatenate([jnp.where(low, q2, zero), jnp.where(low, zero, q2)], axis=0)
            scores = lax.dot_general(
                stacked, k2, (((1,), (1,)), ((), ())), preferred_element_type=F32
            ) * SCALE
            scores = jnp.where(allowed, scores, MASKED)
            grown = jnp.exp(scores - jnp.max(scores, axis=-1, keepdims=True))
            weights = (grown / jnp.sum(grown, axis=-1, keepdims=True)).astype(BF16)
            both = jnp.dot(weights, v2, preferred_element_type=F32)
            mix[b, :, j * pair:(j + 1) * pair] = jnp.where(low, both[:seq], both[seq:]).astype(BF16)

    def step_z(b, c):
        with jax.named_scope("z_wait"):
            sum_x(b, 0, c).wait_recv()
        zs[b, :, strip(c)] = (pf[quarter(z_q), strip(c)] + rx[b, :rows, strip(c)].astype(F32)).astype(BF16)
        sum_z(b, c).start()

    def step_y(b, c):
        with jax.named_scope("y_wait"):
            sum_x(b, 1, c).wait_recv()
            sum_z(b, c).wait_recv()
        total = (
            pf[quarter(own_q), strip(c)] + rx[b, rows:, strip(c)].astype(F32)
            + rz[b, :, strip(c)].astype(F32)
        )
        yb[b, :rows, strip(c)] = (arr[b, quarter(own_q), strip(c)].astype(F32) + total).astype(BF16)
        relay_first(b, c).start()

    def step_y2(b, c):
        with jax.named_scope("y_wait"):
            sum_half(b, c).wait_recv()
        mine = side_rows(xl)
        total = pf[mine, strip(c)] + rx[b, :, strip(c)].astype(F32)

        @pl.when(sect == 2)
        def _():
            yb[b, :, strip(c)] = (tg[b, mine, strip(c)].astype(F32) + total).astype(BF16)

        @pl.when(sect != 2)
        def _():
            yb[b, :, strip(c)] = (arr[b, mine, strip(c)].astype(F32) + total).astype(BF16)

        @pl.when(sect < last)
        def _():
            relay(b, c).start()

        if c == CHUNKS - 1:
            @pl.when(sect == last)
            def _():
                def one(t, carry):
                    @pl.when((t != s) | swap)
                    def _():
                        out_copy(b, t).start()

                    @pl.when((t == s) & jnp.logical_not(swap))
                    def _():
                        pltpu.make_async_copy(
                            yb.at[b, :, own_cols],
                            out.at[b, pl.ds(pl.multiple_of(xl * half, half), half)], out_r.at[b],
                        ).start()
                    return carry

                lax.fori_loop(0, n_seg, one, 0)

    @pl.when(swap)
    def _():
        lens_copy().wait()
        lens[...] = lens_far[...]

    @pl.when(jnp.logical_not(swap))
    def _():
        lens[...] = lens_own[...]

    with jax.named_scope("load"):
        load_in.wait()
        load_out.wait()

    @pl.when(sect == 2)
    def _():
        def first(b, carry):
            wait_for(tg.at[b, quarter(own_q)], tgt_r.at[b])
            target_z(b).start()
            target_x(b, 0).start()
            return carry

        lax.fori_loop(0, batches, first, 0)

        def second(b, carry):
            target_z(b).wait_recv()
            target_x(b, 1).start()
            return carry

        lax.fori_loop(0, batches, second, 0)

        def third(b, carry):
            target_x(b, 0).wait_recv()
            target_x(b, 1).wait_recv()
            nb[...] = rms(tg[b].astype(F32), own_gain).astype(BF16)
            qs[b] = jnp.dot(nb[...], w_in[:, :heads], preferred_element_type=F32).astype(BF16)
            return carry

        with jax.named_scope("target_q"):
            lax.fori_loop(0, batches, third, 0)

    @pl.when(upper)
    def _():
        with jax.named_scope("far"):
            far_copy().wait_recv()
            for k in range(1, tall):
                far_side(k).start()
            for k in range(1, tall):
                wait_for(w_far.at[far_rows((y + tall - k) % tall)], far_r.at[k])
            far_swap().start()

    @pl.when(sect == 0)
    def _():
        step_r(0)
        for c in range(CHUNKS):
            step_f(0, c)

    @pl.when(upper)
    def _():
        for c in range(CHUNKS):
            step_f2(0, c)
        far_swap().wait_recv()

    def main(b, carry):
        more = b < batches - 1

        @pl.when(lower)
        def _():
            for c in range(CHUNKS):
                step_r2(b, c)

        with jax.named_scope("c_wait"):
            @pl.when(sect == 0)
            def _():
                for c in range(CHUNKS):
                    gather_x(b, 0, c).wait_recv()
                    gather_x(b, 1, c).wait_recv()

            @pl.when(sect > 0)
            def _():
                for c in range(CHUNKS):
                    half_x(b, c).wait_recv()

        @pl.when(more & (sect == 0))
        def _():
            step_r(b + 1)

        attend(b)

        @pl.when(lower)
        def _():
            mix_z(b).start()

        @pl.when(sect == 0)
        def _():
            for c in range(CHUNKS):
                with jax.named_scope("out_dot"):
                    total = jnp.dot(mix[b], w_out[:, strip(c)], preferred_element_type=F32)
                    pf[:, strip(c)] = total
                    part[b, :, strip(c)] = total.astype(BF16)
                sum_x(b, 0, c).start()
                sum_x(b, 1, c).start()

            @pl.when(more)
            def _():
                for c in range(CHUNKS):
                    step_f(b + 1, c)

            for c in range(CHUNKS):
                step_z(b, c)
            for c in range(CHUNKS):
                step_y(b, c)

        @pl.when(upper)
        def _():
            @pl.when(more)
            def _():
                for c in range(EARLY):
                    step_f2(b + 1, c)

            with jax.named_scope("mix_wait"):
                mix_z(b).wait_recv()
            for c in range(CHUNKS):
                with jax.named_scope("out_dot2"):
                    total = jnp.dot(mix[b], w_out[:, strip(c)], preferred_element_type=F32)
                    total = total + jnp.dot(mix_far[b], w_far[:, strip(c)], preferred_element_type=F32)
                    pf[:, strip(c)] = total
                    part[b, :, strip(c)] = total.astype(BF16)
                sum_half(b, c).start()

            @pl.when(more)
            def _():
                for c in range(EARLY, AHEAD):
                    step_f2(b + 1, c)

            for c in range(CHUNKS):
                if c + AHEAD < CHUNKS:
                    @pl.when(more)
                    def _():
                        step_f2(b + 1, c + AHEAD)

                step_y2(b, c)
        return carry

    lax.fori_loop(0, batches, main, 0)

    def finish(b, carry):
        @pl.when((sect == 0) | (b > 0))
        def _():
            scattered(src, arr, src_s, src_r, 0, b)

        scattered(tgt, tg, tgt_s, tgt_r, 2 * GROUP, b)
        for c in range(CHUNKS):
            @pl.when(sect == 0)
            def _():
                sum_x(b, 0, c).wait_send()
                sum_x(b, 1, c).wait_send()
                sum_z(b, c).wait_send()
                gather_z(b, c).wait_send()
                gather_x(b, 0, c).wait_send()
                gather_x(b, 1, c).wait_send()
                relay_first(b, c).wait_send()

            @pl.when(lower)
            def _():
                lift_z(b, c).wait_send()
                half_x(b, c).wait_send()

            @pl.when(upper)
            def _():
                half_x(b, c).wait_send()
                sum_half(b, c).wait_send()

            @pl.when(upper & (sect < last))
            def _():
                relay(b, c).wait_send()

        @pl.when(lower)
        def _():
            mix_z(b).wait_send()

        @pl.when(sect == 2)
        def _():
            target_z(b).wait_send()
            target_x(b, 0).wait_send()
            target_x(b, 1).wait_send()

        @pl.when(upper & (sect == last))
        def _():
            def one(t, inner):
                @pl.when((t != s) | swap)
                def _():
                    out_copy(b, t).wait_send()
                return inner

            lax.fori_loop(0, n_seg, one, 0)

        with jax.named_scope("o_wait"):
            wait_for(out.at[b], out_r.at[b])
        return carry

    lax.fori_loop(0, batches, finish, 0)

    @pl.when(lower)
    def _():
        far_copy().wait_send()

    @pl.when(upper)
    def _():
        far_swap().wait_send()
        for k in range(1, tall):
            far_side(k).wait_send()


def on_device(n_seg, n_dp, src, tgt, slen, tlen, win, wout, gain, fgain):
    batches, seq, cols = src.shape
    width = cols * n_seg
    depth, fan = win.shape[1:]
    heads = wout.shape[1]
    rows = seq // GROUP
    any_space = pl.BlockSpec(memory_space=pl.ANY)
    vmem = pl.BlockSpec(memory_space=pltpu.VMEM)
    smem = pl.BlockSpec(memory_space=pltpu.SMEM)
    dma = pltpu.SemaphoreType.DMA
    return pl.pallas_call(
        functools.partial(kernel, n_seg, n_dp),
        out_shape=jax.ShapeDtypeStruct((batches, seq, cols), BF16),
        in_specs=[any_space, any_space, smem, smem, any_space, any_space, vmem, vmem],
        out_specs=any_space,
        scratch_shapes=[
            pltpu.VMEM((depth, fan), BF16),
            pltpu.VMEM((heads, width), BF16),
            pltpu.VMEM((heads, width), BF16),
            pltpu.VMEM((2 * batches, 128), F32),
            pltpu.VMEM((2 * batches, 128), F32),
            pltpu.VMEM((2 * batches, 128), F32),
            pltpu.VMEM((batches, seq, width), BF16),
            pltpu.VMEM((batches, seq, width), BF16),
            pltpu.VMEM((seq, width), BF16),
            pltpu.VMEM((batches, seq, heads), BF16),
            pltpu.VMEM((seq, fan), BF16),
            pltpu.VMEM((batches, seq, heads), BF16),
            pltpu.VMEM((batches, seq, heads), BF16),
            pltpu.VMEM((seq, width), F32),
            pltpu.VMEM((batches, seq, width), BF16),
            pltpu.VMEM((batches, 2 * rows, width), BF16),
            pltpu.VMEM((batches, rows, width), BF16),
            pltpu.VMEM((batches, rows, width), BF16),
            pltpu.VMEM((batches, 2 * rows, width), BF16),
            dma((2,)), dma, dma, dma((n_dp // 4 + 1,)), dma((n_dp // 4 + 1,)), dma((batches,)), dma((batches,)),
            dma((batches, GROUP)), dma((batches, GROUP)), dma((batches,)), dma((batches,)),
            dma((batches,)), dma((batches,)), dma((batches, 2)), dma((batches, 2)),
            dma((batches, CHUNKS)), dma((batches, CHUNKS)),
            dma((batches, CHUNKS)), dma((batches, CHUNKS)),
            dma((batches, 2, CHUNKS)), dma((batches, 2, CHUNKS)),
            dma((batches, 2, CHUNKS)), dma((batches, 2, CHUNKS)),
            dma((batches, CHUNKS)), dma((batches, CHUNKS)),
            dma((batches, n_seg)), dma((batches,)),
        ],
        compiler_params=pltpu.CompilerParams(
            collective_id=0, has_side_effects=True, vmem_limit_bytes=56 * 1024 * 1024
        ),
    )(src, tgt, slen, tlen, win, wout, gain, fgain.reshape(1, -1))


def solution(mesh):
    spec = P("dp", None, "segment")
    return jax.shard_map(
        functools.partial(on_device, mesh.shape["segment"], mesh.shape["dp"]),
        mesh=mesh,
        in_specs=(spec, spec, P("dp"), P("dp"), P("segment", None, None), P("segment", None, None), P(), P()),
        out_specs=spec,
        check_vma=False,
    )
```

profile of v0, /device:TPU:32, one launch (start us, length us, event | category | flops | bytes accessed | tf_op | source)
XLA Modules:
  0.0 140.2 jit_solution(10265986883908144339)
XLA Ops:
  0.0 138.6 %shard_map.82 = bf16[4,128,128]{2,1,0:T(8,128)(2,1)} custom-call(bf16[4,128,128]{2,1,0:T(8,128)(2,1)} %src.1, bf16[4,128,128]{2,1,0:T(8,128)(2,1)} %tgt.1, s32[4]{0:T(128)} %slen.1, s32[4]{0:T(128)} %tlen.1, bf16[1,2048,1536]{2,1,0:T(8,128)(2,1)} %win.1, bf16[1,512,2048]{2,1,0:T(8,128)(2,1)} %wout.1, f32[4,2048]{1,0:T(4,128)} %gain.1, f32[1,2048]{1,0:T(1,128)} %bitcast.1), custom_call_target="tpu_custom_call" | custom-call | tf_op jit(solution)/shard_map/pallas_call | solution.py:602
  138.6 1.6 %copy.10 = bf16[4,128,128]{2,1,0:T(8,128)(2,1)} copy(bf16[4,128,128]{2,1,0:T(8,128)(2,1)} %shard_map.82) | data formatting | bytes 262144
where the time goes:
time: 140 us
  Pallas kernels  139 us (99%)
  local copies, waits for them, and re-layouts  1.57 us (1%)
    pallas_call x1, Pallas kernels, on_device(): pl.pallas_call(functools.partial(kernel, n_seg, n_dp), out_shape=jax.Shap...  139 us

commit v1 on v0

--- a/solution.py
+++ b/solution.py
@@ -26,8 +26,8 @@
 
 def kernel(
     n_seg, n_dp, src, tgt, slen, tlen, win, wout, gain, fgain, out,
-    w_in, w_out, w_far, lens_own, lens_far, lens, arr, tg, nb, qs, qkv, mix, mix_far, pf, part, rx, rz, zs, yb,
-    wsem, lens_s, lens_r, far_s, far_r, mix_s, mix_r, src_s, tgt_s, src_r, tgt_r, tz_s, tz_r, tx_s, tx_r,
+    w_in, w_out, w_far, lens_own, lens_far, lens, arr, tg, nb, qs, acc, qkv, mix, mix_far, pf, part, rx, rz, zs, yb,
+    go, wsem, lens_s, lens_r, far_s, far_r, mix_s, mix_r, src_s, tgt_s, src_r, tgt_r, tz_s, tz_r, tx_s, tx_r,
     relay_s, relay_r, agz_s, agz_r, agx_s, agx_r, rsx_s, rsx_r, rsz_s, rsz_r, out_s, out_r,
 ):
     batches, seq, cols = src.shape
@@ -44,7 +44,7 @@
     d = lax.axis_index("dp")
     flipped = d + 2 - 4 * ((d // 2) % 2)
     alt = d % 2 == 1
-    swap = alt & (xl == 0)
+    swap = alt & (xl == 1)
     x_dp = jnp.where(alt, flipped, d)
     work_dp = jnp.where(swap, flipped, d)
     core = d % 2
@@ -66,11 +66,9 @@
         pl.semaphore_signal(
             barrier, inc=1, device_id={"segment": (s + k) % n_seg}, device_id_type=MESH
         )
-
     pl.semaphore_signal(
         barrier, inc=1, device_id={"segment": s, "dp": twin}, device_id_type=MESH
     )
-
     for k in range(1, n_dp // 4):
         pl.semaphore_signal(
             barrier, inc=1, device_id={"segment": s, "dp": (d + 4 * k) % n_dp}, device_id_type=MESH
@@ -142,12 +140,12 @@
         return remote(
             given.at[b, part_of(t)], held.at[b, part_of(t), own_cols],
             send.at[b, t], recv.at[b], first + t,
-            jnp.where(alt, flipped, d) if t % 2 == 0 else d,
+            jnp.where(alt, flipped, d) if t % 2 == 1 else d,
         )
 
     def stays(first, t):
         same = s == first + t
-        return same & jnp.logical_not(alt) if t % 2 == 0 else same
+        return same & jnp.logical_not(alt) if t % 2 == 1 else same
 
     def scatter(given, held, send, recv, first, b):
         for t in range(GROUP):
@@ -176,22 +174,66 @@
         far_copy().start()
 
     give_source(0, 0)
-
-    @pl.when(sect > 0)
-    def _():
-        scattered(src, arr, src_s, src_r, 0, 0)
-
-    lax.fori_loop(1, batches, give_source, 0)
-
-    @pl.when(lower & (sect > 1))
-    def _():
-        far_copy().start()
+    give_source(1, 0)
 
     def give_target(b, carry):
         scatter(tgt, tg, tgt_s, tgt_r, 2 * GROUP, b)
         return carry
 
-    lax.fori_loop(0, batches, give_target, 0)
+    def paced(b, carry):
+        give_source(b, carry)
+        scattered(src, arr, src_s, src_r, 0, b)
+        return carry
+
+    @pl.when(sect == 0)
+    def _():
+        with jax.named_scope("first_wait"):
+            wait_for(arr.at[0, quarter(own_q)], src_r.at[0])
+
+    @pl.when(sect > 0)
+    def _():
+        scattered(src, arr, src_s, src_r, 0, 0)
+        scattered(src, arr, src_s, src_r, 0, 1)
+        lax.fori_loop(0, batches, give_target, 0)
+
+    @pl.when(lower & (sect == 2))
+    def _():
+        far_copy().start()
+
+    def far_share():
+        with jax.named_scope("far"):
+            far_copy().wait_recv()
+            for k in range(1, tall):
+                far_side(k).start()
+
+    @pl.when(upper & (sect < last))
+    def _():
+        far_share()
+
+    @pl.when(sect > 0)
+    def _():
+        with jax.named_scope("go_wait"):
+            pl.semaphore_wait(go, GROUP)
+
+    @pl.when(sect == 1)
+    def _():
+        lax.fori_loop(2, batches, give_source, 0)
+
+    @pl.when(sect > 1)
+    def _():
+        with jax.named_scope("paced"):
+            lax.fori_loop(2, batches, paced, 0)
+
+    @pl.when(lower & (sect > 2))
+    def _():
+        far_copy().start()
+
+    def go_ahead():
+        for k in range(GROUP, n_seg):
+            pl.semaphore_signal(
+                go, inc=1, device_id={"segment": k, "dp": work_dp}, device_id_type=MESH
+            )
+        lax.fori_loop(2, batches, give_source, 0)
 
     def side_rows(side):
         return pl.ds(pl.multiple_of(side * half, half), half)
@@ -257,9 +299,10 @@
             out.at[b, pl.ds(pl.multiple_of(xl * half, half), half)], out_s.at[b, t], out_r.at[b], t, work_dp,
         )
 
-    def step_r(b):
-        with jax.named_scope("r_wait"):
-            wait_for(arr.at[b, quarter(own_q)], src_r.at[b])
+    def step_r(b, waits=True):
+        if waits:
+            with jax.named_scope("r_wait"):
+                wait_for(arr.at[b, quarter(own_q)], src_r.at[b])
         for c in range(CHUNKS):
             gather_z(b, c).start()
             gather_x(b, 0, c).start()
@@ -282,24 +325,30 @@
 
     own_gain = gain[pl.ds(sect, 1), :]
 
+    strip_gain = jnp.where(sect == 2, fgain[...], own_gain)
+
+    def project(b, wait):
+        squares = jnp.zeros((seq, 1), F32)
+        for c in range(CHUNKS):
+            wait(c)
+            held = arr[b, :, strip(c)].astype(F32)
+            squares = squares + jnp.sum(held * held, axis=-1, keepdims=True)
+            nb[:, strip(c)] = (held * strip_gain[:, strip(c)]).astype(BF16)
+            with jax.named_scope("kv_dot"):
+                grown = jnp.dot(nb[:, strip(c)], w_in[strip(c), :], preferred_element_type=F32)
+                if c == 0:
+                    acc[...] = grown
+                elif c < CHUNKS - 1:
+                    acc[...] += grown
+                else:
+                    scale = lax.rsqrt(squares / (cols * n_seg) + EPS)
+                    qkv[...] = ((acc[...] + grown) * scale).astype(BF16)
+
+        @pl.when(sect == 2)
+        def _():
+            qkv[:, :heads] = qs[b]
+
     def attend(b):
-        @pl.when(sect == 2)
-        def _():
-            qkv[:, :heads] = qs[b]
-            nb[...] = rms(arr[b].astype(F32), fgain[...]).astype(BF16)
-
-        @pl.when(sect != 2)
-        def _():
-            nb[...] = rms(arr[b].astype(F32), own_gain).astype(BF16)
-            qkv[:, :heads] = jnp.dot(
-                nb[...], w_in[:, :heads], preferred_element_type=F32
-            ).astype(BF16)
-
-        with jax.named_scope("kv_dot"):
-            qkv[:, heads:] = jnp.dot(
-                nb[...], w_in[:, heads:], preferred_element_type=F32
-            ).astype(BF16)
-
         length = lens[pl.ds(jnp.where(sect == last, batches, 0) + b, 1), :seq]
         query_pos = lax.broadcasted_iota(jnp.int32, (seq, seq), 0)
         key_pos = lax.broadcasted_iota(jnp.int32, (seq, seq), 1)
@@ -399,6 +448,12 @@
 
         lax.fori_loop(0, batches, first, 0)
 
+    @pl.when(upper & (sect == last))
+    def _():
+        far_share()
+
+    @pl.when(sect == 2)
+    def _():
         def second(b, carry):
             target_z(b).wait_recv()
             target_x(b, 1).start()
@@ -418,19 +473,18 @@
 
     @pl.when(upper)
     def _():
-        with jax.named_scope("far"):
-            far_copy().wait_recv()
-            for k in range(1, tall):
-                far_side(k).start()
+        with jax.named_scope("far_side"):
             for k in range(1, tall):
                 wait_for(w_far.at[far_rows((y + tall - k) % tall)], far_r.at[k])
             far_swap().start()
 
     @pl.when(sect == 0)
     def _():
-        step_r(0)
+        step_r(0, False)
+        lax.fori_loop(0, batches, give_target, 0)
         for c in range(CHUNKS):
             step_f(0, c)
+        step_r(1)
 
     @pl.when(upper)
     def _():
@@ -446,22 +500,26 @@
             for c in range(CHUNKS):
                 step_r2(b, c)
 
-        with jax.named_scope("c_wait"):
-            @pl.when(sect == 0)
-            def _():
-                for c in range(CHUNKS):
+        @pl.when(more & (sect == 0) & (b > 0))
+        def _():
+            step_r(b + 1)
+
+        def arrived(c):
+            with jax.named_scope("c_wait"):
+                @pl.when(sect == 0)
+                def _():
                     gather_x(b, 0, c).wait_recv()
                     gather_x(b, 1, c).wait_recv()
 
-            @pl.when(sect > 0)
-            def _():
-                for c in range(CHUNKS):
+                @pl.when(sect > 0)
+                def _():
                     half_x(b, c).wait_recv()
 
-        @pl.when(more & (sect == 0))
-        def _():
-            step_r(b + 1)
-
+        project(b, arrived)
+
+        @pl.when((sect == 0) & (b == 0))
+        def _():
+            go_ahead()
         attend(b)
 
         @pl.when(lower)
@@ -476,6 +534,7 @@
                     pf[:, strip(c)] = total
                     part[b, :, strip(c)] = total.astype(BF16)
                 sum_x(b, 0, c).start()
+            for c in range(CHUNKS):
                 sum_x(b, 1, c).start()
 
             @pl.when(more)
@@ -505,24 +564,28 @@
                     part[b, :, strip(c)] = total.astype(BF16)
                 sum_half(b, c).start()
 
-            @pl.when(more)
-            def _():
-                for c in range(EARLY, AHEAD):
-                    step_f2(b + 1, c)
-
-            for c in range(CHUNKS):
-                if c + AHEAD < CHUNKS:
+            @pl.when(b == 0)
+            def _():
+                for c in range(CHUNKS):
+                    step_y2(b, c)
+                    if c > 0:
+                        step_f2(b + 1, c - 1)
+                step_f2(b + 1, CHUNKS - 1)
+
+            @pl.when(b > 0)
+            def _():
+                for c in range(CHUNKS):
                     @pl.when(more)
                     def _():
-                        step_f2(b + 1, c + AHEAD)
-
-                step_y2(b, c)
+                        step_f2(b + 1, c)
+
+                    step_y2(b, c)
         return carry
 
     lax.fori_loop(0, batches, main, 0)
 
     def finish(b, carry):
-        @pl.when((sect == 0) | (b > 0))
+        @pl.when((sect == 0) | ((sect == 1) & (b > 1)))
         def _():
             scattered(src, arr, src_s, src_r, 0, b)
 
@@ -615,6 +678,7 @@
             pltpu.VMEM((batches, seq, width), BF16),
             pltpu.VMEM((seq, width), BF16),
             pltpu.VMEM((batches, seq, heads), BF16),
+            pltpu.VMEM((seq, fan), F32),
             pltpu.VMEM((seq, fan), BF16),
             pltpu.VMEM((batches, seq, heads), BF16),
             pltpu.VMEM((batches, seq, heads), BF16),
@@ -624,7 +688,7 @@
             pltpu.VMEM((batches, rows, width), BF16),
             pltpu.VMEM((batches, rows, width), BF16),
             pltpu.VMEM((batches, 2 * rows, width), BF16),
-            dma((2,)), dma, dma, dma((n_dp // 4 + 1,)), dma((n_dp // 4 + 1,)), dma((batches,)), dma((batches,)),
+            pltpu.SemaphoreType.REGULAR, dma((2,)), dma, dma, dma((n_dp // 4 + 1,)), dma((n_dp // 4 + 1,)), dma((batches,)), dma((batches,)),
             dma((batches, GROUP)), dma((batches, GROUP)), dma((batches,)), dma((batches,)),
             dma((batches,)), dma((batches,)), dma((batches, 2)), dma((batches, 2)),
             dma((batches, CHUNKS)), dma((batches, CHUNKS)),

time: 140 us -> 133 us (0.950)
  Pallas kernels: 139 us -> 132 us
    pallas_call x1, Pallas kernels: 139 us -> 132 us  [on_device(): pl.pallas_call(functools.partial(kernel, n_seg, n_dp), out_shape=jax.Shap...]
where the time goes in v1:
time: 133 us
  Pallas kernels  132 us (99%)
  local copies, waits for them, and re-layouts  1.57 us (1%)
    pallas_call x1, Pallas kernels, on_device(): pl.pallas_call(functools.partial(kernel, n_seg, n_dp), out_shape=jax.Shap...  132 us

profile of v1, /device:TPU:32, one launch (start us, length us, event | category | flops | bytes accessed | tf_op | source)
XLA Modules:
  0.0 133.1 jit_solution(14683042311446338807)
XLA Ops:
  0.0 131.5 %shard_map.82 = bf16[4,128,128]{2,1,0:T(8,128)(2,1)} custom-call(bf16[4,128,128]{2,1,0:T(8,128)(2,1)} %src.1, bf16[4,128,128]{2,1,0:T(8,128)(2,1)} %tgt.1, s32[4]{0:T(128)} %slen.1, s32[4]{0:T(128)} %tlen.1, bf16[1,2048,1536]{2,1,0:T(8,128)(2,1)} %win.1, bf16[1,512,2048]{2,1,0:T(8,128)(2,1)} %wout.1, f32[4,2048]{1,0:T(4,128)} %gain.1, f32[1,2048]{1,0:T(1,128)} %bitcast.1), custom_call_target="tpu_custom_call" | custom-call | tf_op jit(solution)/shard_map/pallas_call | solution.py:665
  131.6 1.6 %copy.10 = bf16[4,128,128]{2,1,0:T(8,128)(2,1)} copy(bf16[4,128,128]{2,1,0:T(8,128)(2,1)} %shard_map.82) | data formatting | bytes 262144

commit v2 on v1

--- a/solution.py
+++ b/solution.py
@@ -9,7 +9,7 @@
 
 HEAD = 64
 GROUP = 4
-CHUNKS = 4
+CHUNKS = 8
 AHEAD = 1
 EARLY = 0
 EPS = 1e-06
@@ -266,8 +266,11 @@
         ref = arr.at[b, side_rows(xl), strip(c)]
         return remote(ref, ref, agx_s.at[b, 0, c], agx_r.at[b, 0, c], x_near, x_dp)
 
-    def mix_z(b):
-        return remote(mix.at[b], mix_far.at[b], mix_s.at[b], mix_r.at[b], z_near)
+    def mix_z(b, k):
+        side = slice(k * heads // 2, (k + 1) * heads // 2)
+        return remote(
+            mix.at[b, :, side], mix_far.at[b, :, side], mix_s.at[b, k], mix_r.at[b, k], z_near
+        )
 
     def target_z(b):
         ref = tg.at[b, quarter(own_q)]
@@ -295,7 +298,7 @@
 
     def out_copy(b, t):
         return remote(
-            yb.at[b, :, pl.ds(pl.multiple_of(t * cols, cols), cols)],
+            yb.at[b, :, pl.ds(t * cols if isinstance(t, int) else pl.multiple_of(t * cols, cols), cols)],
             out.at[b, pl.ds(pl.multiple_of(xl * half, half), half)], out_s.at[b, t], out_r.at[b], t, work_dp,
         )
 
@@ -371,6 +374,10 @@
             weights = (grown / jnp.sum(grown, axis=-1, keepdims=True)).astype(BF16)
             both = jnp.dot(weights, v2, preferred_element_type=F32)
             mix[b, :, j * pair:(j + 1) * pair] = jnp.where(low, both[:seq], both[seq:]).astype(BF16)
+            if (j + 1) * pair * 2 == heads:
+                @pl.when(lower)
+                def _():
+                    mix_z(b, 0).start()
 
     def step_z(b, c):
         with jax.named_scope("z_wait"):
@@ -407,23 +414,19 @@
         def _():
             relay(b, c).start()
 
-        if c == CHUNKS - 1:
-            @pl.when(sect == last)
-            def _():
-                def one(t, carry):
-                    @pl.when((t != s) | swap)
-                    def _():
-                        out_copy(b, t).start()
-
-                    @pl.when((t == s) & jnp.logical_not(swap))
-                    def _():
-                        pltpu.make_async_copy(
-                            yb.at[b, :, own_cols],
-                            out.at[b, pl.ds(pl.multiple_of(xl * half, half), half)], out_r.at[b],
-                        ).start()
-                    return carry
-
-                lax.fori_loop(0, n_seg, one, 0)
+        @pl.when(sect == last)
+        def _():
+            for t in range(c * n_seg // CHUNKS, (c + 1) * n_seg // CHUNKS):
+                @pl.when((t != s) | swap)
+                def _():
+                    out_copy(b, t).start()
+
+                @pl.when((t == s) & jnp.logical_not(swap))
+                def _():
+                    pltpu.make_async_copy(
+                        yb.at[b, :, own_cols],
+                        out.at[b, pl.ds(pl.multiple_of(xl * half, half), half)], out_r.at[b],
+                    ).start()
 
     @pl.when(swap)
     def _():
@@ -524,7 +527,7 @@
 
         @pl.when(lower)
         def _():
-            mix_z(b).start()
+            mix_z(b, 1).start()
 
         @pl.when(sect == 0)
         def _():
@@ -555,7 +558,8 @@
                     step_f2(b + 1, c)
 
             with jax.named_scope("mix_wait"):
-                mix_z(b).wait_recv()
+                mix_z(b, 0).wait_recv()
+                mix_z(b, 1).wait_recv()
             for c in range(CHUNKS):
                 with jax.named_scope("out_dot2"):
                     total = jnp.dot(mix[b], w_out[:, strip(c)], preferred_element_type=F32)
@@ -617,7 +621,8 @@
 
         @pl.when(lower)
         def _():
-            mix_z(b).wait_send()
+            mix_z(b, 0).wait_send()
+            mix_z(b, 1).wait_send()
 
         @pl.when(sect == 2)
         def _():
@@ -688,7 +693,7 @@
             pltpu.VMEM((batches, rows, width), BF16),
             pltpu.VMEM((batches, rows, width), BF16),
             pltpu.VMEM((batches, 2 * rows, width), BF16),
-            pltpu.SemaphoreType.REGULAR, dma((2,)), dma, dma, dma((n_dp // 4 + 1,)), dma((n_dp // 4 + 1,)), dma((batches,)), dma((batches,)),
+            pltpu.SemaphoreType.REGULAR, dma((2,)), dma, dma, dma((n_dp // 4 + 1,)), dma((n_dp // 4 + 1,)), dma((batches, 2)), dma((batches, 2)),
             dma((batches, GROUP)), dma((batches, GROUP)), dma((batches,)), dma((batches,)),
             dma((batches,)), dma((batches,)), dma((batches, 2)), dma((batches, 2)),
             dma((batches, CHUNKS)), dma((batches, CHUNKS)),

time: 133 us -> 131 us (0.985)
  Pallas kernels: 132 us -> 128 us
    pallas_call x1, Pallas kernels: 132 us -> 128 us  [on_device(): pl.pallas_call(functools.partial(kernel, n_seg, n_dp), out_shape=jax.Shap...]
where the time goes in v2:
time: 131 us; the launch traced here: 130 us
  Pallas kernels  128 us (98%)
  local copies, waits for them, and re-layouts  1.57 us (1%)
    pallas_call x1, Pallas kernels, on_device(): pl.pallas_call(functools.partial(kernel, n_seg, n_dp), out_shape=jax.Shap...  128 us

profile of v2, /device:TPU:32, one launch (start us, length us, event | category | flops | bytes accessed | tf_op | source)
XLA Modules:
  0.0 130.0 jit_solution(7188789518680356581)
XLA Ops:
  0.0 128.4 %shard_map.82 = bf16[4,128,128]{2,1,0:T(8,128)(2,1)} custom-call(bf16[4,128,128]{2,1,0:T(8,128)(2,1)} %src.1, bf16[4,128,128]{2,1,0:T(8,128)(2,1)} %tgt.1, s32[4]{0:T(128)} %slen.1, s32[4]{0:T(128)} %tlen.1, bf16[1,2048,1536]{2,1,0:T(8,128)(2,1)} %win.1, bf16[1,512,2048]{2,1,0:T(8,128)(2,1)} %wout.1, f32[4,2048]{1,0:T(4,128)} %gain.1, f32[1,2048]{1,0:T(1,128)} %bitcast.1), custom_call_target="tpu_custom_call" | custom-call | tf_op jit(solution)/shard_map/pallas_call | solution.py:670
  128.4 1.6 %copy.10 = bf16[4,128,128]{2,1,0:T(8,128)(2,1)} copy(bf16[4,128,128]{2,1,0:T(8,128)(2,1)} %shard_map.82) | data formatting | bytes 262144

commit v3 on v2

--- a/solution.py
+++ b/solution.py
@@ -10,6 +10,8 @@
 HEAD = 64
 GROUP = 4
 CHUNKS = 8
+WIDE = 4
+PROJ = 4
 AHEAD = 1
 EARLY = 0
 EPS = 1e-06
@@ -27,7 +29,7 @@
 def kernel(
     n_seg, n_dp, src, tgt, slen, tlen, win, wout, gain, fgain, out,
     w_in, w_out, w_far, lens_own, lens_far, lens, arr, tg, nb, qs, acc, qkv, mix, mix_far, pf, part, rx, rz, zs, yb,
-    go, wsem, lens_s, lens_r, far_s, far_r, mix_s, mix_r, src_s, tgt_s, src_r, tgt_r, tz_s, tz_r, tx_s, tx_r,
+    go, turn, wsem, lens_s, lens_r, far_s, far_r, mix_s, mix_r, src_s, tgt_s, src_r, tgt_r, tz_s, tz_r, tx_s, tx_r,
     relay_s, relay_r, agz_s, agz_r, agx_s, agx_r, rsx_s, rsx_r, rsz_s, rsz_r, out_s, out_r,
 ):
     batches, seq, cols = src.shape
@@ -113,6 +115,12 @@
     def strip(c):
         return slice(c * block, (c + 1) * block)
 
+    def wide(c, pieces):
+        return slice(c * cols * n_seg // pieces, (c + 1) * cols * n_seg // pieces)
+
+    def strips_of(c, pieces):
+        return range(c * CHUNKS // pieces, (c + 1) * CHUNKS // pieces)
+
     tall = n_dp // 4
     share = heads // (2 * tall)
     y = d // 4
@@ -332,16 +340,18 @@
 
     def project(b, wait):
         squares = jnp.zeros((seq, 1), F32)
-        for c in range(CHUNKS):
-            wait(c)
-            held = arr[b, :, strip(c)].astype(F32)
+        for w in range(PROJ):
+            for c in strips_of(w, PROJ):
+                wait(c)
+            span = wide(w, PROJ)
+            held = arr[b, :, span].astype(F32)
             squares = squares + jnp.sum(held * held, axis=-1, keepdims=True)
-            nb[:, strip(c)] = (held * strip_gain[:, strip(c)]).astype(BF16)
+            nb[:, span] = (held * strip_gain[:, span]).astype(BF16)
             with jax.named_scope("kv_dot"):
-                grown = jnp.dot(nb[:, strip(c)], w_in[strip(c), :], preferred_element_type=F32)
-                if c == 0:
+                grown = jnp.dot(nb[:, span], w_in[span, :], preferred_element_type=F32)
+                if w == 0:
                     acc[...] = grown
-                elif c < CHUNKS - 1:
+                elif w < PROJ - 1:
                     acc[...] += grown
                 else:
                     scale = lax.rsqrt(squares / (cols * n_seg) + EPS)
@@ -518,6 +528,16 @@
                 def _():
                     half_x(b, c).wait_recv()
 
+        @pl.when((sect == 0) & (b > 0) & (core == 0))
+        def _():
+            pl.semaphore_signal(
+                turn, inc=1, device_id={"segment": s, "dp": twin}, device_id_type=MESH
+            )
+
+        @pl.when((sect == 0) & (b > 0) & (core == 1))
+        def _():
+            pl.semaphore_wait(turn, 1)
+
         project(b, arrived)
 
         @pl.when((sect == 0) & (b == 0))
@@ -531,14 +551,16 @@
 
         @pl.when(sect == 0)
         def _():
-            for c in range(CHUNKS):
+            for w in range(WIDE):
                 with jax.named_scope("out_dot"):
-                    total = jnp.dot(mix[b], w_out[:, strip(c)], preferred_element_type=F32)
-                    pf[:, strip(c)] = total
-                    part[b, :, strip(c)] = total.astype(BF16)
-                sum_x(b, 0, c).start()
+                    total = jnp.dot(mix[b], w_out[:, wide(w, WIDE)], preferred_element_type=F32)
+                    pf[:, wide(w, WIDE)] = total
+                    part[b, :, wide(w, WIDE)] = total.astype(BF16)
+                for c in strips_of(w, WIDE):
+                    sum_x(b, 0, c).start()
             for c in range(CHUNKS):
                 sum_x(b, 1, c).start()
+
 
             @pl.when(more)
             def _():
@@ -560,13 +582,14 @@
             with jax.named_scope("mix_wait"):
                 mix_z(b, 0).wait_recv()
                 mix_z(b, 1).wait_recv()
-            for c in range(CHUNKS):
+            for w in range(WIDE):
                 with jax.named_scope("out_dot2"):
-                    total = jnp.dot(mix[b], w_out[:, strip(c)], preferred_element_type=F32)
-                    total = total + jnp.dot(mix_far[b], w_far[:, strip(c)], preferred_element_type=F32)
-                    pf[:, strip(c)] = total
-                    part[b, :, strip(c)] = total.astype(BF16)
-                sum_half(b, c).start()
+                    total = jnp.dot(mix[b], w_out[:, wide(w, WIDE)], preferred_element_type=F32)
+                    total = total + jnp.dot(mix_far[b], w_far[:, wide(w, WIDE)], preferred_element_type=F32)
+                    pf[:, wide(w, WIDE)] = total
+                    part[b, :, wide(w, WIDE)] = total.astype(BF16)
+                for c in strips_of(w, WIDE):
+                    sum_half(b, c).start()
 
             @pl.when(b == 0)
             def _():
@@ -693,7 +716,7 @@
             pltpu.VMEM((batches, rows, width), BF16),
             pltpu.VMEM((batches, rows, width), BF16),
             pltpu.VMEM((batches, 2 * rows, width), BF16),
-            pltpu.SemaphoreType.REGULAR, dma((2,)), dma, dma, dma((n_dp // 4 + 1,)), dma((n_dp // 4 + 1,)), dma((batches, 2)), dma((batches, 2)),
+            pltpu.SemaphoreType.REGULAR, pltpu.SemaphoreType.REGULAR, dma((2,)), dma, dma, dma((n_dp // 4 + 1,)), dma((n_dp // 4 + 1,)), dma((batches, 2)), dma((batches, 2)),
             dma((batches, GROUP)), dma((batches, GROUP)), dma((batches,)), dma((batches,)),
             dma((batches,)), dma((batches,)), dma((batches, 2)), dma((batches, 2)),
             dma((batches, CHUNKS)), dma((batches, CHUNKS)),

time: 131 us -> 131 us (level)
  no operation moved by 1% of the time
where the time goes in v3:
time: 131 us; the launch traced here: 130 us
  Pallas kernels  128 us (98%)
  local copies, waits for them, and re-layouts  1.57 us (1%)
    pallas_call x1, Pallas kernels, on_device(): pl.pallas_call(functools.partial(kernel, n_seg, n_dp), out_shape=jax.Shap...  128 us

profile of v3, /device:TPU:32, one launch (start us, length us, event | category | flops | bytes accessed | tf_op | source)
XLA Modules:
  0.0 129.6 jit_solution(10226396214073594043)
XLA Ops:
  0.0 128.0 %shard_map.82 = bf16[4,128,128]{2,1,0:T(8,128)(2,1)} custom-call(bf16[4,128,128]{2,1,0:T(8,128)(2,1)} %src.1, bf16[4,128,128]{2,1,0:T(8,128)(2,1)} %tgt.1, s32[4]{0:T(128)} %slen.1, s32[4]{0:T(128)} %tlen.1, bf16[1,2048,1536]{2,1,0:T(8,128)(2,1)} %win.1, bf16[1,512,2048]{2,1,0:T(8,128)(2,1)} %wout.1, f32[4,2048]{1,0:T(4,128)} %gain.1, f32[1,2048]{1,0:T(1,128)} %bitcast.1), custom_call_target="tpu_custom_call" | custom-call | tf_op jit(solution)/shard_map/pallas_call | solution.py:693
  128.0 1.6 %copy.10 = bf16[4,128,128]{2,1,0:T(8,128)(2,1)} copy(bf16[4,128,128]{2,1,0:T(8,128)(2,1)} %shard_map.82) | data formatting | bytes 262144

commit v4 on v3

--- a/solution.py
+++ b/solution.py
@@ -528,13 +528,13 @@
                 def _():
                     half_x(b, c).wait_recv()
 
-        @pl.when((sect == 0) & (b > 0) & (core == 0))
+        @pl.when(((sect == 0) | (lower & (sect == 2))) & (b > 0) & (core == 0))
         def _():
             pl.semaphore_signal(
                 turn, inc=1, device_id={"segment": s, "dp": twin}, device_id_type=MESH
             )
 
-        @pl.when((sect == 0) & (b > 0) & (core == 1))
+        @pl.when(((sect == 0) | (lower & (sect == 2))) & (b > 0) & (core == 1))
         def _():
             pl.semaphore_wait(turn, 1)
 

time: 131 us -> 131 us (level)
  no operation moved by 1% of the time
where the time goes in v4:
time: 131 us; the launch traced here: 130 us
  Pallas kernels  129 us (98%)
  local copies, waits for them, and re-layouts  1.57 us (1%)
    pallas_call x1, Pallas kernels, on_device(): pl.pallas_call(functools.partial(kernel, n_seg, n_dp), out_shape=jax.Shap...  129 us

profile of v4, /device:TPU:32, one launch (start us, length us, event | category | flops | bytes accessed | tf_op | source)
XLA Modules:
  0.0 130.5 jit_solution(268468938558749824)
XLA Ops:
  0.0 128.9 %shard_map.82 = bf16[4,128,128]{2,1,0:T(8,128)(2,1)} custom-call(bf16[4,128,128]{2,1,0:T(8,128)(2,1)} %src.1, bf16[4,128,128]{2,1,0:T(8,128)(2,1)} %tgt.1, s32[4]{0:T(128)} %slen.1, s32[4]{0:T(128)} %tlen.1, bf16[1,2048,1536]{2,1,0:T(8,128)(2,1)} %win.1, bf16[1,512,2048]{2,1,0:T(8,128)(2,1)} %wout.1, f32[4,2048]{1,0:T(4,128)} %gain.1, f32[1,2048]{1,0:T(1,128)} %bitcast.1), custom_call_target="tpu_custom_call" | custom-call | tf_op jit(solution)/shard_map/pallas_call | solution.py:693
  128.9 1.6 %copy.10 = bf16[4,128,128]{2,1,0:T(8,128)(2,1)} copy(bf16[4,128,128]{2,1,0:T(8,128)(2,1)} %shard_map.82) | data formatting | bytes 262144
